TPU v7x, 256 devices: a whole 4x4x8 slice. The times are simulated.
256 devices in a mesh: pipe: 8 (over x, z_lo), tensor: 4 (over y), expert: 8 (over z_hi, core).
Axes of the slice: x: 4, y: 4, z: 8 (z_hi: 4, z_lo: 2; z = z_hi * 2 + z_lo), core: 2. Of those that a mesh axis runs over, the one named last changes fastest.
Arguments:
- tokens: bfloat16 [2, 512, 4096], P(None, 'expert'), may hold values from -6 to 6
- gains: float32 [8, 4096], P('pipe'), may hold values from 0.1 to 1.9
- route_ids: int32 [8, 2, 512, 2], P('pipe', None, 'expert'), may hold values from 0 to 7, all different within a row
- route_weights: float32 [8, 2, 512, 2], P('pipe', None, 'expert'), may hold values from 0.2 to 1
- picks: int32 [8, 2, 8, 64], P('pipe', None, 'expert'), may hold values from 0 to 63, each once within a row
- w_gate: bfloat16 [8, 8, 4096, 1536], P('pipe', 'expert', None, 'tensor'), may hold values from -0.09375 to 0.09375
- w_up: bfloat16 [8, 8, 4096, 1536], P('pipe', 'expert', None, 'tensor'), may hold values from -0.09375 to 0.09375
- w_down: bfloat16 [8, 8, 1536, 4096], P('pipe', 'expert', 'tensor'), may hold values from -0.15625 to 0.15625
Outputs:
- streams: bfloat16 [8, 2, 512, 4096], P('pipe', None, 'expert', 'tensor')
Inputs may be any that keep to these rules, and one draw needn't show every extreme that they name: `route_ids`: each token names 2 different experts; every expert is named by some token. `picks`: for every layer, micro-batch and block of 64 tokens, a permutation of 0 to 63.
All inputs are finite; a program needn't handle non-finite values.
Results may differ from a plain program's by a relative error of at most 0.025.
Values may be sent and summed in bfloat16 or wider, within the bound.
A program may use at most 64 MiB of HBM per device.

v0:
```python
import functools

import jax
import jax.numpy as jnp
from jax import lax
from jax.experimental import pallas as pl
from jax.experimental.pallas import tpu as pltpu
from jax.sharding import PartitionSpec as P

epsilon = 1e-06
MESH = pl.DeviceIdType.MESH
F32 = jnp.float32
BF16 = jnp.bfloat16


def layer_kernel(
    sizes, tokens, gains, ids, weights, picks, w_gate, w_up, w_down, out,
    placing, comb, h_in, fresh, send, x, wg, wu, wd, g_acc, u_acc, own, p_send, p_recv,
    y_send, y_recv, z_send, ret,
    w_sem, h_loc, h_send, h_recv, d_send, d_recv, f_send, f_recv, c_send, c_recv,
    ps_sem, pr_sem, ys_sem, yr_sem, zs_sem, zr_sem,
):
    micros, n_p, n_t, n_e, pair, rows_ge, width, capacity = sizes
    n_a = n_t // pair
    cut = (n_e + 1) // 2
    halves = [list(range(cut)), list(range(n_e - 1, cut - 1, -1))]
    p = lax.axis_index("pipe")
    r = lax.axis_index("tensor")
    z = lax.axis_index("expert")
    a = lax.div(r, pair)
    c = lax.rem(r, pair)

    def peer_e(d):
        other = z
        for bit in range(n_e.bit_length()):
            one = 1 << bit
            if d & one:
                other = other + one * (1 - 2 * lax.rem(lax.div(z, one), 2))
        return other

    def rank_of(da, dc):
        return lax.rem(a + da, n_a) * pair + lax.rem(c + dc, pair)

    def remote(src, dst, ssem, rsem, where):
        return pltpu.make_async_remote_copy(
            src_ref=src, dst_ref=dst, send_sem=ssem, recv_sem=rsem,
            device_id=where, device_id_type=MESH,
        )

    loads = [
        pltpu.make_async_copy(w_gate.at[0, 0], wg, w_sem.at[0]),
        pltpu.make_async_copy(w_up.at[0, 0], wu, w_sem.at[1]),
        pltpu.make_async_copy(w_down.at[0, 0], wd, w_sem.at[2]),
    ]

    def first_load(m):
        cols = pl.ds(pl.multiple_of(r * width, width), width)
        return pltpu.make_async_copy(tokens.at[m, :, cols], h_in.at[m], h_loc.at[m])

    @pl.when(p == 0)
    def _():
        for m in range(micros):
            first_load(m).start()

    for load in loads:
        load.start()

    barrier = pltpu.get_barrier_semaphore()

    def greet(where):
        pl.semaphore_signal(barrier, inc=1, device_id=where, device_id_type=MESH)

    for d in range(1, n_e):
        greet({"expert": peer_e(d)})
    for da in range(1, n_a):
        greet({"tensor": rank_of(da, 0)})
    for dc in range(1, pair):
        greet({"tensor": rank_of(0, dc)})

    @pl.when(p > 0)
    def _():
        greet({"pipe": p - 1})

    @pl.when(p < n_p - 1)
    def _():
        greet({"pipe": p + 1})

    toks = h_in.shape[1]
    quarter = toks // n_t
    down = lax.broadcasted_iota(jnp.int32, (toks, toks), 0)
    across = lax.broadcasted_iota(jnp.int32, (toks, toks), 1)
    same = down == across

    def column(row):
        return jnp.sum(jnp.where(same, row, jnp.zeros_like(row)), axis=1, keepdims=True)

    def row_of(col):
        return jnp.sum(jnp.where(same, col, jnp.zeros_like(col)), axis=0, keepdims=True)

    def slots(m):
        pos = jnp.sum(jnp.where(picks[m] == down, across, 0), axis=1, keepdims=True)
        pos_row = row_of(pos)
        block = lax.div(pos, quarter)
        before = (lax.div(pos_row, quarter) == block) & (pos_row < pos)
        found = []
        for e in range(n_e):
            named = jnp.zeros((1, toks), jnp.int32)
            for k in range(ids.shape[1]):
                named = named + jnp.where(ids[m, k:k + 1] == e, 1, 0)
            slot = jnp.sum(jnp.where(before, named, 0), axis=1, keepdims=True)
            kept = (column(named) > 0) & (slot < capacity)
            found.append(jnp.where(kept, block * capacity + slot, -1))
        return found

    def place(m, targets):
        places = lax.broadcasted_iota(jnp.int32, (rows_ge, toks), 0)
        for e, target in enumerate(targets):
            placing[m, e] = jnp.where(places == row_of(target), 1.0, 0.0).astype(BF16)

    def weigh(m, targets):
        for e, target in enumerate(targets):
            w_row = jnp.zeros((1, toks), F32)
            for k in range(ids.shape[1]):
                w_row = w_row + jnp.where(ids[m, k:k + 1] == e, weights[m, k:k + 1], 0.0)
            spread = lax.broadcasted_iota(jnp.int32, (toks, rows_ge), 1) == target
            w_col = jnp.where(spread, column(w_row), 0.0)
            high = w_col.astype(BF16)
            comb[m, e, :toks] = high
            comb[m, e, toks:] = (w_col - high.astype(F32)).astype(BF16)

    place(0, slots(0))

    ends = jnp.where(p > 0, 1, 0) + jnp.where(p < n_p - 1, 1, 0)
    pl.semaphore_wait(barrier, n_e - 1 + n_a - 1 + pair - 1 + ends)

    def relay(m):
        return remote(fresh.at[m], h_in.at[m], h_send.at[m], h_recv.at[m],
                      {"pipe": jnp.minimum(p + 1, n_p - 1)})

    def d_copy(m, d):
        return remote(send.at[m, d], x.at[m, r, z], d_send.at[m, d], d_recv.at[m, d],
                      {"expert": peer_e(d)})

    def f_copy(m, d, da):
        block = x.at[m, r, peer_e(d)]
        return remote(block, block, f_send.at[m, d, da], f_recv.at[m, d, da],
                      {"tensor": rank_of(da, 0)})

    def c_copy(m, d, da):
        block = x.at[m, rank_of(da, 0), peer_e(d)]
        return remote(block, block, c_send.at[m, d, da], c_recv.at[m, d, da],
                      {"tensor": rank_of(0, 1)})

    def p_copy(m, h, da):
        return remote(p_send.at[m, h, da], p_recv.at[m, h, da], ps_sem.at[m, h, da],
                      pr_sem.at[m, h, da], {"tensor": rank_of(0, 1)})

    def y_copy(m, d, da):
        return remote(y_send.at[m, d, da], y_recv.at[m, d, da], ys_sem.at[m, d, da],
                      yr_sem.at[m, d, da], {"tensor": rank_of(da, 0)})

    def z_copy(m, d):
        return remote(z_send.at[m, d], ret.at[m, z], zs_sem.at[m, d], zr_sem.at[m, d],
                      {"expert": peer_e(d)})

    def dispatch(m):
        @pl.when(p == 0)
        def _():
            first_load(m).wait()

        @pl.when(p > 0)
        def _():
            relay(m).wait_recv()

        h = h_in[m]
        for d in halves[0][1:] + halves[1] + [0]:
            block = jnp.dot(placing[m, peer_e(d)], h, preferred_element_type=F32).astype(BF16)
            if d:
                send[m, d] = block
                d_copy(m, d).start()
            else:
                x[m, r, z] = block

    def forward(m, d):
        if d:
            d_copy(m, d).wait_recv()
        for da in range(1, n_a):
            f_copy(m, d, da).start()
        if pair > 1:
            c_copy(m, d, 0).start()

    def pass_on(m, d):
        for da in range(1, n_a):
            f_copy(m, d, da).wait_recv()
            if pair > 1:
                c_copy(m, d, da).start()

    def compute(m, h):
        if m == 0 and h == 0:
            for load in loads:
                load.wait()
        if pair > 1:
            for d in halves[h]:
                for da in range(n_a):
                    c_copy(m, d, da).wait_recv()
        homes = [peer_e(d) for d in halves[h]]

        def rows_of(q):
            return jnp.concatenate([x[m, q, g].astype(F32) for g in homes], axis=0)

        ss = jnp.zeros((len(homes) * rows_ge, 1), F32)
        for q in range(n_t):
            xf = rows_of(q)
            ss = ss + jnp.sum(xf * xf, axis=-1, keepdims=True)
        inv = lax.rsqrt(ss * (1.0 / (n_t * width)) + epsilon)
        for q in range(n_t):
            cols = slice(q * width, (q + 1) * width)
            nq = (rows_of(q) * inv * gains[0:1, cols]).astype(BF16)
            gq = jnp.dot(nq, wg[cols, :], preferred_element_type=F32)
            uq = jnp.dot(nq, wu[cols, :], preferred_element_type=F32)
            if q == 0:
                g_acc[...] = gq
                u_acc[...] = uq
            else:
                g_acc[...] += gq
                u_acc[...] += uq
        gate = g_acc[...]
        hidden = (gate / (1.0 + jnp.exp(-gate)) * u_acc[...]).astype(BF16)
        for dc in list(range(1, pair)) + [0]:
            for da in list(range(1, n_a)) + [0]:
                start = pl.multiple_of(rank_of(da, dc) * width, width)
                part = jnp.dot(hidden, wd[:, pl.ds(start, width)], preferred_element_type=F32)
                if dc:
                    p_send[m, h, da] = part.astype(BF16)
                    p_copy(m, h, da).start()
                else:
                    own[m, h, da] = part.astype(BF16)

    def reduce_pair(m, h):
        for da in list(range(1, n_a)) + [0]:
            if pair > 1:
                p_copy(m, h, da).wait_recv()
            for i, d in enumerate(halves[h]):
                part = slice(i * rows_ge, (i + 1) * rows_ge)
                total = own[m, h, da, part].astype(F32)
                if pair > 1:
                    total = total + p_recv[m, h, da, part].astype(F32)
                y_send[m, d, da] = total.astype(BF16)
                if da and d:
                    y_copy(m, d, da).start()
            if h and da:
                y_copy(m, 0, da).start()

    def reduce_far(m, d):
        total = y_send[m, d, 0].astype(F32)
        for da in range(1, n_a):
            y_copy(m, d, da).wait_recv()
            total = total + y_recv[m, d, da].astype(F32)
        if d:
            z_send[m, d] = total.astype(BF16)
            z_copy(m, d).start()
        else:
            ret[m, z] = total.astype(BF16)

    def combine(m):
        for d in halves[0] + halves[1]:
            e = peer_e(d)
            if d:
                z_copy(m, d).wait_recv()
            both = jnp.dot(comb[m, e], ret[m, e], preferred_element_type=F32)
            g_part = both[:toks] + both[toks:]
            update = g_part if d == 0 else update + g_part
        new = (h_in[m].astype(F32) + update).astype(BF16)
        fresh[m] = new
        out[0, m] = new

        @pl.when(p < n_p - 1)
        def _():
            relay(m).start()

    first, second = halves

    def step(fn, *args):
        return functools.partial(fn, *args)

    def when(test, fn, *args):
        pl.when(test)(functools.partial(fn, *args))

    def head(m):
        steps = [step(forward, m, d) for d in first]
        steps += [step(pass_on, m, d) for d in first[:-1]]
        steps += [step(forward, m, second[0]), step(pass_on, m, first[-1])]
        if m:
            steps += [step(when, p == 0, forward, m, d) for d in second[1:]]
        return steps

    def middle(m):
        steps = [step(compute, m, 0)]
        if m:
            steps += [step(when, p > 0, forward, m, d) for d in second[1:]]
        else:
            steps += [step(forward, m, d) for d in second[1:]]
        steps += [step(pass_on, m, d) for d in second[:-1]]
        steps += [step(reduce_pair, m, 0), step(pass_on, m, second[-1])]
        return steps

    def back(m):
        return [step(compute, m, 1), step(reduce_pair, m, 1)]

    def tail(m):
        return [step(reduce_far, m, d) for d in first[1:] + second + first[:1]]

    def both_of(one, two):
        mixed = []
        for i in range(max(len(one), len(two))):
            mixed += one[i:i + 1] + two[i:i + 1]
        return mixed

    dispatch(0)
    head(0)[0]()
    for m in range(1, micros):
        place(m, slots(m))

    @pl.when(p == 0)
    def _():
        for m in range(1, micros):
            dispatch(m)

    for m in range(micros):
        weigh(m, slots(m))

    def late_dispatch(m):
        @pl.when(p > 0)
        def _():
            dispatch(m)

    plan = head(0)[1:]
    for m in range(micros):
        plan += middle(m)
        if m:
            plan += [step(when, p < n_p - 1, combine, m - 1)]
        plan += back(m)
        if m + 1 < micros:
            plan += [step(late_dispatch, m + 1)]
            plan += both_of(tail(m), head(m + 1))
    plan += tail(micros - 1)
    plan += [step(when, p == n_p - 1, combine, m) for m in range(micros - 1)]
    plan += [step(combine, micros - 1)]
    for go in plan:
        go()

    for m in range(micros):
        for d in range(n_e):
            if d:
                d_copy(m, d).wait_send()
                z_copy(m, d).wait_send()
            for da in range(n_a):
                if da:
                    f_copy(m, d, da).wait_send()
                    y_copy(m, d, da).wait_send()
                if pair > 1:
                    c_copy(m, d, da).wait_send()
        if pair > 1:
            for h in range(len(halves)):
                for da in range(n_a):
                    p_copy(m, h, da).wait_send()

        @pl.when(p < n_p - 1)
        def _():
            relay(m).wait_send()


def local(mesh_shape, tokens, gains, route_ids, route_weights, picks, w_gate, w_up, w_down):
    n_p, n_t, n_e = mesh_shape
    micros, toks, model_width = tokens.shape
    route_count = route_ids.shape[3]
    quarter = toks // n_t
    capacity = 4 * quarter * route_count // (3 * n_e)
    width = model_width // n_t
    pair = 2 if n_t % 2 == 0 else 1
    n_a = n_t // pair
    rows_ge = -(-n_t * capacity // 8) * 8
    cut = (n_e + 1) // 2
    rows = cut * rows_ge
    hidden_width = w_gate.shape[3]

    ids = route_ids[0].transpose(0, 2, 1)
    weights = route_weights[0].transpose(0, 2, 1)
    order = picks[0]

    sizes = (micros, n_p, n_t, n_e, pair, rows_ge, width, capacity)
    dma = pltpu.SemaphoreType.DMA
    vmem = pl.BlockSpec(memory_space=pltpu.VMEM)
    anywhere = pl.BlockSpec(memory_space=pl.ANY)
    return pl.pallas_call(
        functools.partial(layer_kernel, sizes),
        out_shape=jax.ShapeDtypeStruct((1, micros, toks, width), BF16),
        in_specs=[anywhere, vmem, vmem, vmem, vmem, anywhere, anywhere, anywhere],
        out_specs=vmem,
        scratch_shapes=[
            pltpu.VMEM((micros, n_e, rows_ge, toks), BF16),
            pltpu.VMEM((micros, n_e, 2 * toks, rows_ge), BF16),
            pltpu.VMEM((micros, toks, width), BF16),
            pltpu.VMEM((micros, toks, width), BF16),
            pltpu.VMEM((micros, n_e, rows_ge, width), BF16),
            pltpu.VMEM((micros, n_t, n_e, rows_ge, width), BF16),
            pltpu.VMEM(w_gate.shape[2:], BF16),
            pltpu.VMEM(w_up.shape[2:], BF16),
            pltpu.VMEM(w_down.shape[2:], BF16),
            pltpu.VMEM((rows, hidden_width), F32),
            pltpu.VMEM((rows, hidden_width), F32),
            pltpu.VMEM((micros, 2, n_a, rows, width), BF16),
            pltpu.VMEM((micros, 2, n_a, rows, width), BF16),
            pltpu.VMEM((micros, 2, n_a, rows, width), BF16),
            pltpu.VMEM((micros, n_e, n_a, rows_ge, width), BF16),
            pltpu.VMEM((micros, n_e, n_a, rows_ge, width), BF16),
            pltpu.VMEM((micros, n_e, rows_ge, width), BF16),
            pltpu.VMEM((micros, n_e, rows_ge, width), BF16),
            dma((3,)), dma((micros,)), dma((micros,)), dma((micros,)),
            dma((micros, n_e)), dma((micros, n_e)),
            dma((micros, n_e, n_a)), dma((micros, n_e, n_a)),
            dma((micros, n_e, n_a)), dma((micros, n_e, n_a)),
            dma((micros, 2, n_a)), dma((micros, 2, n_a)),
            dma((micros, n_e, n_a)), dma((micros, n_e, n_a)),
            dma((micros, n_e)), dma((micros, n_e)),
        ],
        compiler_params=pltpu.CompilerParams(
            collective_id=0, has_side_effects=True, vmem_limit_bytes=67043328 - 600 * 1024
        ),
    )(tokens, gains, ids, weights, order, w_gate, w_up, w_down)


def solution(mesh):
    mesh_shape = (mesh.shape["pipe"], mesh.shape["tensor"], mesh.shape["expert"])
    return jax.shard_map(
        functools.partial(local, mesh_shape),
        mesh=mesh,
        in_specs=(
            P(None, "expert", None),
            P("pipe", None),
            P("pipe", None, "expert", None),
            P("pipe", None, "expert", None),
            P("pipe", None, "expert", None),
            P("pipe", "expert", None, "tensor"),
            P("pipe", "expert", None, "tensor"),
            P("pipe", "expert", "tensor", None),
        ),
        out_specs=P("pipe", None, "expert", "tensor"),
        check_vma=False,
    )
```

profile of v0, /device:TPU:38, one launch (start us, length us, event | category | flops | bytes accessed | tf_op | source)
XLA Modules:
  0.0 790.0 jit_solution(13295519618040561675)
XLA Ops:
  0.0 788.4 %shard_map.82 = bf16[1,2,64,1024]{3,2,1,0:T(8,128)(2,1)} custom-call(bf16[2,64,4096]{2,1,0:T(8,128)(2,1)} %tokens.1, f32[1,4096]{1,0:T(1,128)} %gains.1, s32[2,2,64]{2,1,0:T(2,128)} %bitcast.9, f32[2,2,64]{2,1,0:T(2,128)} %bitcast.10, s32[2,1,64]{2,1,0:T(1,128)} %bitcast.11, bf16[1,1,4096,384]{3,2,1,0:T(8,128)(2,1)} %w_gate.1, ...), custom_call_target="tpu_custom_call" | custom-call | tf_op jit(solution)/shard_map/pallas_call | solution.py:395
  788.4 1.7 copy.11
where the time goes:
time: 790 us
  Pallas kernels  788 us (100%)
    pallas_call x1, Pallas kernels, local(): pl.pallas_call(functools.partial(layer_kernel, sizes), out_shape=jax.Shap...  788 us

commit v1 on v0

v1 whole, which is shorter than its diff:
```python
import functools

import jax
import jax.numpy as jnp
from jax import lax
from jax.experimental import pallas as pl
from jax.experimental.pallas import tpu as pltpu
from jax.sharding import PartitionSpec as P

epsilon = 1e-06
MESH = pl.DeviceIdType.MESH
F32 = jnp.float32
BF16 = jnp.bfloat16
CH = 4
MAIN = 16
REM = 4
BLOCK = CH * (MAIN + REM)


def layer_kernel(
    sizes, tokens, gains, meta, weights, w_gate, w_up, w_down, out,
    nmeta, placing, comb, perm, h_in, fresh, isend, dsend, x, wgu, wdt, acc, sq, hid, yacc, zsend, ret,
    w_sem, wt_send, wt_recv, m_send, m_recv, h_loc, h_send, h_recv, i_send, d_send, d_recv,
    a_send, a_recv, b_send, b_recv, hs_send, hs_recv, hf_send, hf_recv, z_send, z_recv,
):
    micros, n_p, n_t, n_e, capacity, toks, width = sizes
    n_hi = n_e // 2
    lanes = width // CH
    rows = n_e * (MAIN + REM)
    main_rows = n_e * MAIN
    p = lax.axis_index("pipe")
    r = lax.axis_index("tensor")
    z = lax.axis_index("expert")
    z_hi = lax.div(z, 2)
    core = lax.rem(z, 2)
    right = lax.rem(r + 1, n_t)
    left = lax.rem(r + n_t - 1, n_t)
    across_r = lax.rem(r + 2, n_t)

    def diff(j, odd):
        return [0, 1 + 2 * odd, 3 - 2 * odd, 2][j]

    def target(k, odd):
        hi = lax.rem(z_hi + diff(k // 2, odd), n_hi)
        return 2 * hi + (core if k % 2 == 0 else 1 - core)

    def source(k, odd):
        hi = lax.rem(z_hi - diff(k // 2, odd) + n_hi, n_hi)
        return 2 * hi + (core if k % 2 == 0 else 1 - core)

    def remote(src, dst, ssem, rsem, where):
        return pltpu.make_async_remote_copy(
            src_ref=src, dst_ref=dst, send_sem=ssem, recv_sem=rsem,
            device_id=where, device_id_type=MESH,
        )

    def cols_of(q, size):
        return pl.ds(pl.multiple_of(q * size, size), size)

    hidden_width = w_gate.shape[3]
    loads = [
        pltpu.make_async_copy(w_gate.at[0, 0], wgu.at[:, :hidden_width], w_sem.at[0]),
        pltpu.make_async_copy(w_up.at[0, 0], wgu.at[:, hidden_width:], w_sem.at[1]),
        pltpu.make_async_copy(w_down.at[0, 0, :, cols_of(r, width)], wdt.at[r], w_sem.at[2]),
    ]

    def first_load(m, c):
        cols = pl.ds(pl.multiple_of(r * width + c * lanes, lanes), lanes)
        return pltpu.make_async_copy(
            tokens.at[m, :, cols], h_in.at[m, c * toks:(c + 1) * toks], h_loc.at[m, c])

    @pl.when(p == 0)
    def _():
        for m in range(micros):
            for c in range(CH):
                first_load(m, c).start()

    for load in loads:
        load.start()

    barrier = pltpu.get_barrier_semaphore()

    def greet(where):
        pl.semaphore_signal(barrier, inc=1, device_id=where, device_id_type=MESH)

    for d in range(1, n_e):
        greet({"expert": lax.rem(z + d, n_e)})
    for d in range(1, n_t):
        greet({"tensor": lax.rem(r + d, n_t)})

    @pl.when(p > 0)
    def _():
        for e in range(n_e):
            greet({"pipe": p - 1, "expert": e})

    @pl.when(p < n_p - 1)
    def _():
        for e in range(n_e):
            greet({"pipe": p + 1, "expert": e})

    def iota(shape, dim):
        return lax.broadcasted_iota(jnp.int32, shape, dim)

    down = iota((toks, toks), 0)
    across = iota((toks, toks), 1)
    same = down == across
    quarter = toks // n_t

    def column(row):
        return jnp.sum(jnp.where(same, row, jnp.zeros_like(row)), axis=1, keepdims=True)

    def row_of(col):
        return jnp.sum(jnp.where(same, col, jnp.zeros_like(col)), axis=0, keepdims=True)

    def slots(table, m):
        pos = jnp.sum(jnp.where(table[m, 2:3, :toks] == down, across, 0), axis=1, keepdims=True)
        pos_row = row_of(pos)
        block = lax.div(pos, quarter)
        before = (lax.div(pos_row, quarter) == block) & (pos_row < pos)
        found = []
        for e in range(n_e):
            named = jnp.zeros((1, toks), jnp.int32)
            for k in range(2):
                named = named + jnp.where(table[m, k:k + 1, :toks] == e, 1, 0)
            slot = jnp.sum(jnp.where(before, named, 0), axis=1, keepdims=True)
            kept = (column(named) > 0) & (slot < capacity)
            found.append(jnp.where(kept, block * capacity + slot, -1))
        return found

    def place(table, m):
        i = iota((BLOCK, CH * toks), 0)
        is_main = i < CH * MAIN
        key = jnp.where(
            is_main,
            lax.rem(i, MAIN) + 32 * lax.div(i, MAIN),
            MAIN + lax.rem(i, REM) + 32 * lax.div(i - CH * MAIN, REM))
        t_of = lax.rem(iota((toks, CH * toks), 1), toks) == iota((toks, CH * toks), 0)
        shift = 32 * lax.div(iota((1, CH * toks), 1), toks)
        for e, col in enumerate(slots(table, m)):
            wide = jnp.sum(jnp.where(t_of, col, 0), axis=0, keepdims=True) + shift
            placing[m, e] = jnp.where(key == wide, 1.0, 0.0).astype(BF16)

    def weigh(m):
        shape = (toks, 2 * main_rows)
        i = iota(shape, 1)
        is_main = i < main_rows
        of = jnp.where(is_main, lax.div(i, MAIN), lax.div(i - main_rows, CH * REM))
        slot = jnp.where(is_main, lax.rem(i, MAIN), MAIN + lax.rem(i, REM))
        chunk = lax.div(lax.rem(i, CH * REM), REM)
        key = of * 32 + slot
        total = jnp.zeros(shape, F32)
        for e, col in enumerate(slots(meta, m)):
            w_row = jnp.zeros((1, toks), F32)
            for k in range(2):
                w_row = w_row + jnp.where(meta[m, k:k + 1, :toks] == e, weights[m, k:k + 1], 0.0)
            wanted = jnp.where(col < 0, -1, col + 32 * e)
            total = total + jnp.where(key == wanted, column(w_row), 0.0)
        for c in range(CH):
            part = jnp.where(is_main | (chunk == c), total, 0.0)
            high = part.astype(BF16)
            comb[m, c, :toks] = high
            comb[m, c, toks:] = (part - high.astype(F32)).astype(BF16)

    def make_perm():
        n = n_e * CH * REM
        i = iota((n, n), 0)
        j = iota((n, n), 1)
        per = n_e * REM
        there = lax.div(lax.rem(i, per), REM) * (CH * REM) + lax.div(i, per) * REM + lax.rem(i, REM)
        back = lax.div(lax.rem(i, CH * REM), REM) * per + lax.div(i, CH * REM) * REM + lax.rem(i, REM)
        perm[0] = jnp.where(j == there, 1.0, 0.0).astype(BF16)
        perm[1] = jnp.where(j == back, 1.0, 0.0).astype(BF16)

    @pl.when(p == 0)
    def _():
        place(meta, 0)

    ends = jnp.where(p > 0, n_e, 0) + jnp.where(p < n_p - 1, n_e, 0)
    pl.semaphore_wait(barrier, n_e - 1 + n_t - 1 + ends)

    def meta_copy():
        return remote(meta, nmeta, m_send.at[0], m_recv.at[0], {"pipe": jnp.maximum(p - 1, 0)})

    def wt_copy(d):
        there = lax.rem(r + d, n_t)
        return remote(w_down.at[0, 0, :, cols_of(there, width)], wdt.at[r],
                      wt_send.at[d - 1], wt_recv.at[d - 1], {"tensor": there})

    def relay(m):
        return remote(fresh.at[m], h_in.at[m], h_send.at[m], h_recv.at[m],
                      {"pipe": jnp.minimum(p + 1, n_p - 1)})

    def i_copy(m, k):
        e = target(k, 0)
        return remote(isend.at[m, e], x.at[m, r, z], i_send.at[m, k], d_recv.at[m, k], {"expert": e})

    def d_copy(m, k):
        e = target(k, lax.rem(p + 1, 2))
        return remote(dsend.at[m, e], x.at[m, r, z], d_send.at[m, k], d_recv.at[m, k],
                      {"pipe": jnp.minimum(p + 1, n_p - 1), "expert": e})

    def a_copy(m, way, k):
        block = x.at[m, r, source(k, lax.rem(p, 2))]
        return remote(block, block, a_send.at[m, way, k], a_recv.at[m, way, k],
                      {"tensor": left if way else right})

    def b_copy(m, k):
        block = x.at[m, right if k % 2 else left, source(k, lax.rem(p, 2))]
        return remote(block, block, b_send.at[m, k], b_recv.at[m, k],
                      {"tensor": left if k % 2 else right})

    half = rows // 2

    def hs_copy(m, way, k):
        block = hid.at[m, r, k * half:(k + 1) * half]
        return remote(block, block, hs_send.at[m, way, k], hs_recv.at[m, way, k],
                      {"tensor": left if way else right})

    def hf_copy(m, k):
        block = hid.at[m, right if k else left, k * half:(k + 1) * half]
        return remote(block, block, hf_send.at[m, k], hf_recv.at[m, k],
                      {"tensor": left if k else right})

    def z_copy(m, k):
        e = target(k, 0)
        return remote(zsend.at[m, e], ret.at[m, z], z_send.at[m, k], z_recv.at[m, k], {"expert": e})

    def route(m, src, dst, odd, copy):
        h = src[m]
        for j in range(n_hi):
            hi = lax.rem(z_hi + diff(j, odd), n_hi)
            pair = pl.ds(2 * hi, 2)
            both = jnp.dot(placing[m, pair].reshape(2 * BLOCK, CH * toks), h, preferred_element_type=F32)
            dst[m, pair] = both.astype(BF16).reshape(2, BLOCK, lanes)
            for k in (2 * j, 2 * j + 1):
                if copy is i_copy and k == 0:
                    x[m, r, z] = dst[m, z]
                else:
                    copy(m, k).start()

    def own(m, k):
        if k == 0:
            @pl.when(p > 0)
            def _():
                d_copy(m, k).wait_recv()
        else:
            d_copy(m, k).wait_recv()
        for way in range(2):
            a_copy(m, way, k).start()

    def forward(m, k):
        a_copy(m, k % 2, k).wait_recv()
        b_copy(m, k).start()

    def gather_rest(m):
        for k in range(n_e):
            a_copy(m, 1 - k % 2, k).wait_recv()

    def gather_far(m):
        for k in range(n_e):
            b_copy(m, k).wait_recv()

    def project(m, q, first):
        rem = jnp.dot(perm[0], x[m, q, :, CH * MAIN:BLOCK, :].reshape(main_rows, lanes),
                      preferred_element_type=F32)
        per = n_e * REM
        parts = []
        squares = None
        for c in range(CH):
            body = x[m, q, :, c * MAIN:(c + 1) * MAIN, :].reshape(main_rows, lanes).astype(F32)
            full = jnp.concatenate([body, rem[c * per:(c + 1) * per]], axis=0)
            squares = full * full if squares is None else squares + full * full
            parts.append((full * gains[q * CH + c]).astype(BF16))
        both = jnp.dot(jnp.concatenate(parts, axis=1), wgu[cols_of(q, width), :],
                       preferred_element_type=F32)
        if first:
            acc[...] = both
            sq[...] = squares
        else:
            acc[...] += both
            sq[...] += squares

    def hide(m):
        inv = lax.rsqrt(jnp.sum(sq[...], axis=1, keepdims=True) * (1.0 / (n_t * width)) + epsilon)
        gate = acc[:, :hidden_width] * inv
        up = acc[:, hidden_width:] * inv
        hid[m, r] = (gate / (1.0 + jnp.exp(-gate)) * up).astype(BF16)
        for way, k in ((0, 0), (1, 1), (0, 1), (1, 0)):
            hs_copy(m, way, k).start()

    def hid_forward(m):
        for k in range(2):
            hs_copy(m, k, k).wait_recv()
            hf_copy(m, k).start()

    def lower(m, q, first):
        part = jnp.dot(hid[m, q], wdt[q], preferred_element_type=F32)
        if first:
            yacc[...] = part
        else:
            yacc[...] += part

    def give_back(m):
        rem = []
        for c in range(CH):
            part = yacc[:, c * lanes:(c + 1) * lanes].astype(BF16)
            zsend[m, :, c * MAIN:(c + 1) * MAIN, :] = part[:main_rows].reshape(n_e, MAIN, lanes)
            rem.append(part[main_rows:])
        swapped = jnp.dot(perm[1], jnp.concatenate(rem, axis=0), preferred_element_type=F32)
        zsend[m, :, CH * MAIN:BLOCK, :] = swapped.astype(BF16).reshape(n_e, CH * REM, lanes)
        for k in range(n_e - 1, 0, -1):
            z_copy(m, k).start()
        ret[m, z] = zsend[m, z]

    def combine(m):
        @pl.when(p > 0)
        def _():
            relay(m).wait_recv()
        for k in range(1, n_e):
            z_copy(m, k).wait_recv()
        last = ret[m, :, CH * MAIN:BLOCK, :].reshape(main_rows, lanes)
        for c in range(CH):
            got = jnp.concatenate(
                [ret[m, :, c * MAIN:(c + 1) * MAIN, :].reshape(main_rows, lanes), last], axis=0)
            both = jnp.dot(comb[m, c], got, preferred_element_type=F32)
            span = slice(c * toks, (c + 1) * toks)
            new = (h_in[m, span].astype(F32) + (both[:toks] + both[toks:])).astype(BF16)
            fresh[m, span] = new
            out[0, m, :, c * lanes:(c + 1) * lanes] = new

        @pl.when(p < n_p - 1)
        def _():
            route(m, fresh, dsend, lax.rem(p + 1, 2), d_copy)
            relay(m).start()

    @pl.when(p == 0)
    def _():
        for m in range(micros):
            if m:
                place(meta, m)
            for c in range(CH):
                first_load(m, c).wait()
            route(m, h_in, isend, 0, i_copy)

    @pl.when(p > 0)
    def _():
        meta_copy().start()

    for d in (1, 3, 2):
        wt_copy(d).start()
    make_perm()
    for m in range(micros):
        weigh(m)

    @pl.when(p < n_p - 1)
    def _():
        meta_copy().wait_recv()
        for m in range(micros):
            place(nmeta, m)

    for m in range(micros):
        for k in range(4):
            own(m, k)
        for k in range(4):
            own(m, k + 4)
            forward(m, k)
        if m == 0:
            loads[0].wait()
            loads[1].wait()
        project(m, r, True)
        for k in range(4, n_e):
            forward(m, k)
        gather_rest(m)
        project(m, left, False)
        project(m, right, False)
        gather_far(m)
        project(m, across_r, False)
        hide(m)
        if m == 0:
            loads[2].wait()
        lower(m, r, True)
        hid_forward(m)
        hs_copy(m, 0, 1).wait_recv()
        hs_copy(m, 1, 0).wait_recv()
        if m == 0:
            for d in (1, 3, 2):
                wt_copy(d).wait_recv()
        lower(m, left, False)
        lower(m, right, False)
        for k in range(2):
            hf_copy(m, k).wait_recv()
        lower(m, across_r, False)
        give_back(m)
        combine(m)

    for d in (1, 3, 2):
        wt_copy(d).wait_send()

    @pl.when(p > 0)
    def _():
        meta_copy().wait_send()

    for m in range(micros):
        for k in range(n_e):
            for way in range(2):
                a_copy(m, way, k).wait_send()
            b_copy(m, k).wait_send()
            if k:
                z_copy(m, k).wait_send()
        for k in range(2):
            for way in range(2):
                hs_copy(m, way, k).wait_send()
            hf_copy(m, k).wait_send()

        @pl.when(p == 0)
        def _():
            for k in range(1, n_e):
                i_copy(m, k).wait_send()

        @pl.when(p < n_p - 1)
        def _():
            for k in range(n_e):
                d_copy(m, k).wait_send()
            relay(m).wait_send()


def local(mesh_shape, tokens, gains, route_ids, route_weights, picks, w_gate, w_up, w_down):
    n_p, n_t, n_e = mesh_shape
    micros, toks, model_width = tokens.shape
    route_count = route_ids.shape[3]
    quarter = toks // n_t
    capacity = 4 * quarter * route_count // (3 * n_e)
    width = model_width // n_t
    lanes = width // CH
    hidden_width = w_gate.shape[3]
    rows = n_e * (MAIN + REM)
    ids = route_ids[0].transpose(0, 2, 1)
    weights = route_weights[0].transpose(0, 2, 1)
    meta = jnp.concatenate([ids, picks[0]], axis=1)
    meta = jnp.pad(meta, ((0, 0), (0, 8 - meta.shape[1]), (0, 128 - toks)))
    gain_rows = gains.reshape(n_t * CH, 1, lanes)

    sizes = (micros, n_p, n_t, n_e, capacity, toks, width)
    dma = pltpu.SemaphoreType.DMA
    vmem = pl.BlockSpec(memory_space=pltpu.VMEM)
    anywhere = pl.BlockSpec(memory_space=pl.ANY)
    return pl.pallas_call(
        functools.partial(layer_kernel, sizes),
        out_shape=jax.ShapeDtypeStruct((1, micros, toks, width), BF16),
        in_specs=[anywhere, vmem, vmem, vmem, anywhere, anywhere, anywhere],
        out_specs=vmem,
        scratch_shapes=[
            pltpu.VMEM(meta.shape, jnp.int32),
            pltpu.VMEM((micros, n_e, BLOCK, CH * toks), BF16),
            pltpu.VMEM((micros, CH, 2 * toks, 2 * n_e * MAIN), BF16),
            pltpu.VMEM((2, n_e * CH * REM, n_e * CH * REM), BF16),
            pltpu.VMEM((micros, CH * toks, lanes), BF16),
            pltpu.VMEM((micros, CH * toks, lanes), BF16),
            pltpu.VMEM((micros, n_e, BLOCK, lanes), BF16),
            pltpu.VMEM((micros, n_e, BLOCK, lanes), BF16),
            pltpu.VMEM((micros, n_t, n_e, BLOCK, lanes), BF16),
            pltpu.VMEM((model_width, 2 * hidden_width), BF16),
            pltpu.VMEM((n_t, hidden_width, width), BF16),
            pltpu.VMEM((rows, 2 * hidden_width), F32),
            pltpu.VMEM((rows, lanes), F32),
            pltpu.VMEM((micros, n_t, rows, hidden_width), BF16),
            pltpu.VMEM((rows, width), F32),
            pltpu.VMEM((micros, n_e, BLOCK, lanes), BF16),
            pltpu.VMEM((micros, n_e, BLOCK, lanes), BF16),
            dma((3,)), dma((3,)), dma((3,)), dma((1,)), dma((1,)),
            dma((micros, CH)), dma((micros,)), dma((micros,)),
            dma((micros, n_e)), dma((micros, n_e)), dma((micros, n_e)),
            dma((micros, 2, n_e)), dma((micros, 2, n_e)), dma((micros, n_e)), dma((micros, n_e)),
            dma((micros, 2, 2)), dma((micros, 2, 2)), dma((micros, 2)), dma((micros, 2)),
            dma((micros, n_e)), dma((micros, n_e)),
        ],
        compiler_params=pltpu.CompilerParams(
            collective_id=0, has_side_effects=True, vmem_limit_bytes=67043328 - 600 * 1024
        ),
    )(tokens, gain_rows, meta, weights, w_gate, w_up, w_down)


def solution(mesh):
    mesh_shape = (mesh.shape["pipe"], mesh.shape["tensor"], mesh.shape["expert"])
    return jax.shard_map(
        functools.partial(local, mesh_shape),
        mesh=mesh,
        in_specs=(
            P(None, "expert", None),
            P("pipe", None),
            P("pipe", None, "expert", None),
            P("pipe", None, "expert", None),
            P("pipe", None, "expert", None),
            P("pipe", "expert", None, "tensor"),
            P("pipe", "expert", None, "tensor"),
            P("pipe", "expert", "tensor", None),
        ),
        out_specs=P("pipe", None, "expert", "tensor"),
        check_vma=False,
    )
```

time: 790 us -> 357 us (0.45)
  Pallas kernels: 788 us -> 353 us
    pallas_call x1, Pallas kernels: 788 us -> 353 us  [local(): pl.pallas_call(functools.partial(layer_kernel, sizes), out_shape=jax.Shap...]
where the time goes in v1:
time: 357 us; the launch traced here: 356 us
  Pallas kernels  353 us (99%)
    pallas_call x1, Pallas kernels, local(): pl.pallas_call(functools.partial(layer_kernel, sizes), out_shape=jax.Shap...  353 us

profile of v1, /device:TPU:38, one launch (start us, length us, event | category | flops | bytes accessed | tf_op | source)
XLA Modules:
  0.0 356.5 jit_solution(13638383609455505744)
XLA Ops:
  0.0 0.7 pad_add_fusion
  0.7 0.6 pad.4.meta
  1.3 353.5 %shard_map.82 = bf16[1,2,64,1024]{3,2,1,0:T(8,128)(2,1)} custom-call(bf16[2,64,4096]{2,1,0:T(8,128)(2,1)} %tokens.1, f32[16,1,256]{2,1,0:T(1,128)} %bitcast.10, s32[2,8,128]{2,1,0:T(8,128)} %pad.4.meta, f32[2,2,64]{2,1,0:T(2,128)} %bitcast.11, bf16[1,1,4096,384]{3,2,1,0:T(8,128)(2,1)} %w_gate.1, bf16[1,1,4096,384]{3,2,1,0:T(8,128)(2,1)} %w_up.1, ...), custom_call_target="tpu_custom_call" | custom-call | tf_op jit(solution)/shard_map/pallas_call | solution.py:447
  354.8 1.7 copy.11

commit v2 on v1

--- a/solution.py
+++ b/solution.py
@@ -14,14 +14,17 @@
 CH = 4
 MAIN = 16
 REM = 4
+SHARE = 160
+PIECES = 2
+HELPERS = (2, 6)
 BLOCK = CH * (MAIN + REM)
 
 
 def layer_kernel(
     sizes, tokens, gains, meta, weights, w_gate, w_up, w_down, out,
-    nmeta, placing, comb, perm, h_in, fresh, isend, dsend, x, wgu, wdt, acc, sq, hid, yacc, zsend, ret,
+    nmeta, placing, comb, perm, h_in, fresh, isend, dsend, x, wgu, wdt, acc, sq, hid, yacc, bounce, zsend, ret,
     w_sem, wt_send, wt_recv, m_send, m_recv, h_loc, h_send, h_recv, i_send, d_send, d_recv,
-    a_send, a_recv, b_send, b_recv, hs_send, hs_recv, hf_send, hf_recv, z_send, z_recv,
+    a_send, a_recv, b_send, b_recv, hs_send, hs_recv, hf_send, hf_recv, u_send, u_recv, v_send, v_recv, z_send, z_recv,
 ):
     micros, n_p, n_t, n_e, capacity, toks, width = sizes
     n_hi = n_e // 2
@@ -97,6 +100,19 @@
     def _():
         for e in range(n_e):
             greet({"pipe": p + 1, "expert": e})
+
+    @pl.when(p == 0)
+    def _():
+        for there in HELPERS:
+            for d in range(n_t):
+                greet({"pipe": there, "tensor": lax.rem(r + d, n_t)})
+
+    helper = (p == HELPERS[0]) | (p == HELPERS[1])
+
+    @pl.when(helper)
+    def _():
+        for d in range(n_t):
+            greet({"pipe": 0, "tensor": lax.rem(r + d, n_t)})
 
     def iota(shape, dim):
         return lax.broadcasted_iota(jnp.int32, shape, dim)
@@ -176,6 +192,7 @@
         place(meta, 0)
 
     ends = jnp.where(p > 0, n_e, 0) + jnp.where(p < n_p - 1, n_e, 0)
+    ends = ends + jnp.where(p == 0, len(HELPERS) * n_t, 0) + jnp.where(helper, n_t, 0)
     pl.semaphore_wait(barrier, n_e - 1 + n_t - 1 + ends)
 
     def meta_copy():
@@ -186,6 +203,31 @@
         return remote(w_down.at[0, 0, :, cols_of(there, width)], wdt.at[r],
                       wt_send.at[d - 1], wt_recv.at[d - 1], {"tensor": there})
 
+    piece = SHARE // PIECES
+    rest = hidden_width - len(HELPERS) * SHARE
+
+    def u_copy(n, d, c):
+        there = lax.rem(r + d, n_t)
+        part = pl.ds(n * SHARE + c * piece, piece)
+        return remote(w_down.at[0, 0, part, cols_of(there, width)],
+                      bounce.at[d - 1, c * piece:(c + 1) * piece],
+                      u_send.at[n, d - 1, c], u_recv.at[d - 1, c],
+                      {"pipe": HELPERS[n], "tensor": there})
+
+    def v_copy(n, d, c):
+        part = pl.ds(pl.multiple_of(n * SHARE + c * piece, piece), piece)
+        return remote(bounce.at[d - 1, c * piece:(c + 1) * piece],
+                      wdt.at[lax.rem(r - d + n_t, n_t), part],
+                      v_send.at[d - 1, c], v_recv.at[n, d - 1, c], {"pipe": 0})
+
+    def t_copy(d):
+        there = lax.rem(r + d, n_t)
+        part = pl.ds(hidden_width - rest, rest)
+        return remote(w_down.at[0, 0, part, cols_of(there, width)], wdt.at[r, part],
+                      wt_send.at[d - 1], wt_recv.at[d - 1], {"tensor": there})
+
+    helper_rank = jnp.where(p == HELPERS[0], 0, 1)
+
     def relay(m):
         return remote(fresh.at[m], h_in.at[m], h_send.at[m], h_recv.at[m],
                       {"pipe": jnp.minimum(p + 1, n_p - 1)})
@@ -199,15 +241,18 @@
         return remote(dsend.at[m, e], x.at[m, r, z], d_send.at[m, k], d_recv.at[m, k],
                       {"pipe": jnp.minimum(p + 1, n_p - 1), "expert": e})
 
-    def a_copy(m, way, k):
-        block = x.at[m, r, source(k, lax.rem(p, 2))]
-        return remote(block, block, a_send.at[m, way, k], a_recv.at[m, way, k],
+    def pair_of(j):
+        return pl.ds(2 * lax.rem(z_hi - diff(j, lax.rem(p, 2)) + n_hi, n_hi), 2)
+
+    def a_copy(m, way, j):
+        block = x.at[m, r, pair_of(j)]
+        return remote(block, block, a_send.at[m, way, j], a_recv.at[m, way, j],
                       {"tensor": left if way else right})
 
-    def b_copy(m, k):
-        block = x.at[m, right if k % 2 else left, source(k, lax.rem(p, 2))]
-        return remote(block, block, b_send.at[m, k], b_recv.at[m, k],
-                      {"tensor": left if k % 2 else right})
+    def b_copy(m, j):
+        block = x.at[m, right if j % 2 else left, pair_of(j)]
+        return remote(block, block, b_send.at[m, j], b_recv.at[m, j],
+                      {"tensor": left if j % 2 else right})
 
     half = rows // 2
 
@@ -238,27 +283,28 @@
                 else:
                     copy(m, k).start()
 
-    def own(m, k):
-        if k == 0:
+    def own(m, j):
+        if j == 0:
             @pl.when(p > 0)
             def _():
-                d_copy(m, k).wait_recv()
+                d_copy(m, 0).wait_recv()
         else:
-            d_copy(m, k).wait_recv()
+            d_copy(m, 2 * j).wait_recv()
+        d_copy(m, 2 * j + 1).wait_recv()
         for way in range(2):
-            a_copy(m, way, k).start()
-
-    def forward(m, k):
-        a_copy(m, k % 2, k).wait_recv()
-        b_copy(m, k).start()
+            a_copy(m, way, j).start()
+
+    def forward(m, j):
+        a_copy(m, j % 2, j).wait_recv()
+        b_copy(m, j).start()
 
     def gather_rest(m):
-        for k in range(n_e):
-            a_copy(m, 1 - k % 2, k).wait_recv()
+        for j in range(n_hi):
+            a_copy(m, 1 - j % 2, j).wait_recv()
 
     def gather_far(m):
-        for k in range(n_e):
-            b_copy(m, k).wait_recv()
+        for j in range(n_hi):
+            b_copy(m, j).wait_recv()
 
     def project(m, q, first):
         rem = jnp.dot(perm[0], x[m, q, :, CH * MAIN:BLOCK, :].reshape(main_rows, lanes),
@@ -285,8 +331,6 @@
         gate = acc[:, :hidden_width] * inv
         up = acc[:, hidden_width:] * inv
         hid[m, r] = (gate / (1.0 + jnp.exp(-gate)) * up).astype(BF16)
-        for way, k in ((0, 0), (1, 1), (0, 1), (1, 0)):
-            hs_copy(m, way, k).start()
 
     def hid_forward(m):
         for k in range(2):
@@ -346,8 +390,25 @@
     def _():
         meta_copy().start()
 
-    for d in (1, 3, 2):
-        wt_copy(d).start()
+    @pl.when(p == 0)
+    def _():
+        for d in (1, 3, 2):
+            for c in range(PIECES):
+                for n in range(len(HELPERS)):
+                    u_copy(n, d, c).start()
+
+    @pl.when(helper)
+    def _():
+        for d in (1, 3, 2):
+            for c in range(PIECES):
+                u_copy(0, d, c).wait_recv()
+                v_copy(helper_rank, d, c).start()
+
+    @pl.when(p > 0)
+    def _():
+        for d in (1, 3, 2):
+            wt_copy(d).start()
+
     make_perm()
     for m in range(micros):
         weigh(m)
@@ -358,24 +419,21 @@
         for m in range(micros):
             place(nmeta, m)
 
-    for m in range(micros):
-        for k in range(4):
-            own(m, k)
-        for k in range(4):
-            own(m, k + 4)
-            forward(m, k)
-        if m == 0:
-            loads[0].wait()
-            loads[1].wait()
-        project(m, r, True)
-        for k in range(4, n_e):
-            forward(m, k)
-        gather_rest(m)
-        project(m, left, False)
-        project(m, right, False)
-        gather_far(m)
-        project(m, across_r, False)
-        hide(m)
+    def arrive(d):
+        @pl.when(p > 0)
+        def _():
+            wt_copy(d).wait_recv()
+
+        @pl.when(p == 0)
+        def _():
+            t_copy(d).wait_recv()
+            for c in range(PIECES):
+                for n in range(len(HELPERS)):
+                    v_copy(n, d, c).wait_recv()
+
+    def lower_gathered(m):
+        for way, k in ((0, 0), (1, 1), (0, 1), (1, 0)):
+            hs_copy(m, way, k).start()
         if m == 0:
             loads[2].wait()
         lower(m, r, True)
@@ -383,30 +441,86 @@
         hs_copy(m, 0, 1).wait_recv()
         hs_copy(m, 1, 0).wait_recv()
         if m == 0:
-            for d in (1, 3, 2):
-                wt_copy(d).wait_recv()
+            arrive(1)
         lower(m, left, False)
+        if m == 0:
+            arrive(3)
         lower(m, right, False)
         for k in range(2):
             hf_copy(m, k).wait_recv()
+        if m == 0:
+            arrive(2)
         lower(m, across_r, False)
+
+    def when(test, fn, *args):
+        pl.when(test)(functools.partial(fn, *args))
+
+    def head(m):
+        own(m, 0)
+        own(m, 1)
+        own(m, 2)
+        forward(m, 0)
+        own(m, 3)
+        forward(m, 1)
+
+    def middle(m):
+        if m == 0:
+            loads[0].wait()
+            loads[1].wait()
+        project(m, r, True)
+        forward(m, 2)
+        forward(m, 3)
+
+        if m == 0:
+            @pl.when(p == 0)
+            def _():
+                for d in (1, 3, 2):
+                    t_copy(d).start()
+
+        gather_rest(m)
+        project(m, left, False)
+        project(m, right, False)
+        gather_far(m)
+        project(m, across_r, False)
+        hide(m)
+        lower_gathered(m)
         give_back(m)
+
+    head(0)
+    for m in range(micros):
+        middle(m)
+        if m + 1 < micros:
+            head(m + 1)
         combine(m)
 
-    for d in (1, 3, 2):
-        wt_copy(d).wait_send()
-
     @pl.when(p > 0)
     def _():
         meta_copy().wait_send()
+        for d in (1, 3, 2):
+            wt_copy(d).wait_send()
+
+    @pl.when(p == 0)
+    def _():
+        for d in (1, 3, 2):
+            t_copy(d).wait_send()
+            for c in range(PIECES):
+                for n in range(len(HELPERS)):
+                    u_copy(n, d, c).wait_send()
+
+    @pl.when(helper)
+    def _():
+        for d in (1, 3, 2):
+            for c in range(PIECES):
+                v_copy(helper_rank, d, c).wait_send()
 
     for m in range(micros):
-        for k in range(n_e):
+        for j in range(n_hi):
             for way in range(2):
-                a_copy(m, way, k).wait_send()
-            b_copy(m, k).wait_send()
-            if k:
-                z_copy(m, k).wait_send()
+                a_copy(m, way, j).wait_send()
+            b_copy(m, j).wait_send()
+        for k in range(1, n_e):
+            z_copy(m, k).wait_send()
+
         for k in range(2):
             for way in range(2):
                 hs_copy(m, way, k).wait_send()
@@ -465,13 +579,15 @@
             pltpu.VMEM((rows, lanes), F32),
             pltpu.VMEM((micros, n_t, rows, hidden_width), BF16),
             pltpu.VMEM((rows, width), F32),
+            pltpu.VMEM((n_t - 1, SHARE, width), BF16),
             pltpu.VMEM((micros, n_e, BLOCK, lanes), BF16),
             pltpu.VMEM((micros, n_e, BLOCK, lanes), BF16),
             dma((3,)), dma((3,)), dma((3,)), dma((1,)), dma((1,)),
             dma((micros, CH)), dma((micros,)), dma((micros,)),
             dma((micros, n_e)), dma((micros, n_e)), dma((micros, n_e)),
-            dma((micros, 2, n_e)), dma((micros, 2, n_e)), dma((micros, n_e)), dma((micros, n_e)),
+            dma((micros, 2, n_e // 2)), dma((micros, 2, n_e // 2)), dma((micros, n_e // 2)), dma((micros, n_e // 2)),
             dma((micros, 2, 2)), dma((micros, 2, 2)), dma((micros, 2)), dma((micros, 2)),
+            dma((2, n_t - 1, PIECES)), dma((n_t - 1, PIECES)), dma((n_t - 1, PIECES)), dma((2, n_t - 1, PIECES)),
             dma((micros, n_e)), dma((micros, n_e)),
         ],
         compiler_params=pltpu.CompilerParams(

time: 357 us -> 330 us (0.924)
  Pallas kernels: 353 us -> 326 us
    pallas_call x1, Pallas kernels: 353 us -> 326 us  [local(): pl.pallas_call(functools.partial(layer_kernel, sizes), out_shape=jax.Shap...]
where the time goes in v2:
time: 330 us; the launch traced here: 329 us
  Pallas kernels  326 us (99%)
    pallas_call x1, Pallas kernels, local(): pl.pallas_call(functools.partial(layer_kernel, sizes), out_shape=jax.Shap...  326 us

profile of v2, /device:TPU:38, one launch (start us, length us, event | category | flops | bytes accessed | tf_op | source)
XLA Modules:
  0.0 329.4 jit_solution(10379902464895127583)
XLA Ops:
  0.0 0.7 pad_add_fusion
  0.7 0.6 pad.4.meta
  1.3 326.4 %shard_map.82 = bf16[1,2,64,1024]{3,2,1,0:T(8,128)(2,1)} custom-call(bf16[2,64,4096]{2,1,0:T(8,128)(2,1)} %tokens.1, f32[16,1,256]{2,1,0:T(1,128)} %bitcast.10, s32[2,8,128]{2,1,0:T(8,128)} %pad.4.meta, f32[2,2,64]{2,1,0:T(2,128)} %bitcast.11, bf16[1,1,4096,384]{3,2,1,0:T(8,128)(2,1)} %w_gate.1, bf16[1,1,4096,384]{3,2,1,0:T(8,128)(2,1)} %w_up.1, ...), custom_call_target="tpu_custom_call" | custom-call | tf_op jit(solution)/shard_map/pallas_call | solution.py:561
  327.7 1.7 copy.11
